TPU v7x, 32 devices: a whole 2x2x4 slice. The times are simulated.
32 devices in a mesh: slab: 4 (over z), tile: 8 (over y, x, core).
Axes of the slice: x: 2, y: 2, z: 4, core: 2. Of those that a mesh axis runs over, the one named last changes fastest.
Arguments:
- voxel_grid: float32 [4, 64, 64, 256], P(None, 'slab', 'tile'), may hold values from -4 to 4
- first_moment: float32 [4, 64, 64, 256], P(None, 'slab', 'tile'), may hold values from -0.75 to 0.75
- second_moment: float32 [4, 64, 64, 256], P(None, 'slab', 'tile'), may hold values from 0.01 to 0.5
- pixel_index: int32 [32768], P('tile'), may hold values from 0 to 2047
- start_slab: int32 [32768], P('tile'), may hold values from 0 to 1
- ray_count: int32 [32768], P('tile'), may hold values from 16 to 48
- target: float32 [3, 32768], P(None, 'tile'), may hold values from 0 to 1
Outputs:
- new_grid: float32 [4, 64, 64, 256], P(None, 'slab', 'tile')
- new_first: float32 [4, 64, 64, 256], P(None, 'slab', 'tile')
- new_second: float32 [4, 64, 64, 256], P(None, 'slab', 'tile')
All inputs are finite; a program needn't handle non-finite values.
Results may differ from a plain program's by a relative error of at most 0.0003.
Values sent between devices are 32-bit elements; how exact they have to be, the bound alone decides.
No kernel may reach another device: no remote copies, remote signals or barrier semaphores. Data moves between devices by JAX's collectives and lax.ppermute only.
A program may use at most 128 MiB of HBM per device.

v0:
```python
import math

import jax
import jax.numpy as jnp
from jax import lax
from jax.sharding import PartitionSpec as P

STEP = 20


RENDER_WEIGHT = 1000.0
TV_WEIGHT = 0.05
BACKGROUND = 1.0
STEP_SPAN = 4.0
CLIP_RMS = 0.25
LEARN_RATE = 0.02
BETA_ONE = 0.9
BETA_TWO = 0.99
EPSILON = 1e-08
BLOCK_LIMIT = 1024


def padded_2(cells, sides, width):
    for axis, dim in sides:
        count = lax.axis_size(axis)
        ends = count - 1
        head = lax.slice_in_dim(cells, 0, width, axis=dim)
        tail = lax.slice_in_dim(cells, cells.shape[dim] - width, cells.shape[dim], axis=dim)
        cells = jnp.concatenate(
            [
                lax.ppermute(tail, axis, [(i, (i + 1) % count) for i in range(ends)]),
                cells,
                lax.ppermute(head, axis, [((i + 1) % count, i) for i in range(ends)]),
            ],
            axis=dim,
        )
    return cells


def carried_in(part, axis, combine, identity, reverse):
    count = lax.axis_size(axis)
    place = lax.axis_index(axis)
    ahead = count - 1 - place if reverse else place
    gathered = jax.tree.map(lambda a: lax.all_gather(a, axis), part)
    state = jax.tree.map(lambda a, e: jnp.zeros_like(a) + jnp.asarray(e, a.dtype), part, identity)

    def one(step, state):
        source = count - 1 - step if reverse else step
        return combine(
            state, jax.tree.map(lambda a: lax.dynamic_index_in_dim(a, source, 0, False), gathered)
        )

    return lax.fori_loop(0, ahead, one, state)


def front_join(earlier, later):
    return (earlier[0] + earlier[1][None] * later[0], earlier[1] * later[1])


def back_join(earlier, later):
    return (later[0] + later[1][None] * earlier[0], later[1] * earlier[1])


def per_device(voxel_grid, first_moment, second_moment, pixel_index, start_slab, ray_count, target):
    slab_count = lax.axis_size("slab")
    tile_count = lax.axis_size("tile")
    slab_pos = lax.axis_index("slab")
    tile_pos = lax.axis_index("tile")
    channels, slab_depth, rows_x, rows_y = voxel_grid.shape
    total_depth = slab_depth * slab_count
    total_x = rows_x * tile_count
    pixel_total = rows_x * rows_y
    ray_total = pixel_index.shape[0]
    ray_block = math.gcd(ray_total, BLOCK_LIMIT)
    block_count = ray_total // ray_block
    padded = padded_2(voxel_grid, (("slab", 1), ("tile", 2)), 1)
    depth_pos = slab_pos * slab_depth + jnp.arange(slab_depth, dtype=jnp.int32)
    first_cell = start_slab[None, :] * (total_depth // slab_count)
    inside = (depth_pos[:, None] >= first_cell) & (
        depth_pos[:, None] < first_cell + ray_count[None, :]
    )
    pixel_blocks = pixel_index.reshape(block_count, ray_block)
    pixel_ids = jnp.arange(pixel_total, dtype=jnp.int32)
    depth_ids = jnp.arange(slab_depth, dtype=jnp.int32)
    lower = (depth_ids[:, None] >= depth_ids[None, :]).astype(jnp.float32)

    def march_slab(local_grid):
        flat = local_grid.reshape(channels * slab_depth, pixel_total)

        def pick_block(block_pixels):
            selector = (pixel_ids[:, None] == block_pixels[None, :]).astype(jnp.float32)
            return jnp.dot(
                flat, selector, precision=lax.Precision.HIGHEST, preferred_element_type=jnp.float32
            )

        picked = lax.map(pick_block, pixel_blocks)
        samples = picked.transpose(1, 0, 2).reshape(channels, slab_depth, ray_total)
        optical = jnp.where(inside, jax.nn.softplus(samples[0]) * (STEP_SPAN / total_depth), 0.0)
        running = jnp.dot(
            lower, optical, precision=lax.Precision.HIGHEST, preferred_element_type=jnp.float32
        )
        weights = jnp.exp(-(running - optical)) * (1.0 - jnp.exp(-optical))
        colors = jax.nn.sigmoid(samples[1:4])
        return (jnp.sum(weights[None] * colors, axis=1), jnp.exp(-running[-1]))

    (part_color, part_trans), pullback = jax.vjp(march_slab, voxel_grid)
    empty = (jnp.zeros_like(part_color), jnp.ones_like(part_trans))
    front_color, front_trans = carried_in(
        (part_color, part_trans), "slab", front_join, empty, False
    )
    back_color, back_trans = carried_in((part_color, part_trans), "slab", back_join, empty, True)
    beyond = back_color + back_trans[None] * BACKGROUND
    rendered = front_color + front_trans[None] * (part_color + part_trans[None] * beyond)
    residual = RENDER_WEIGHT * (rendered - target)
    color_cot = front_trans[None] * residual
    trans_cot = front_trans * jnp.sum(residual * beyond, axis=0)
    render_grad = pullback((color_cot, trans_cot))[0]
    depth_view = depth_pos.reshape(1, slab_depth, 1, 1)
    x_view = (tile_pos * rows_x + jnp.arange(rows_x, dtype=jnp.int32)).reshape(1, 1, rows_x, 1)
    smooth = jnp.where(depth_view > 0, voxel_grid - padded[:, :-2, 1:-1, :], 0.0)
    smooth = smooth + jnp.where(
        depth_view < total_depth - 1, voxel_grid - padded[:, 2:, 1:-1, :], 0.0
    )
    smooth = smooth + jnp.where(x_view > 0, voxel_grid - padded[:, 1:-1, :-2, :], 0.0)
    smooth = smooth + jnp.where(x_view < total_x - 1, voxel_grid - padded[:, 1:-1, 2:, :], 0.0)
    step_y = jnp.diff(voxel_grid, axis=3)
    smooth = (
        smooth
        + jnp.pad(-step_y, ((0, 0), (0, 0), (0, 0), (0, 1)))
        + jnp.pad(step_y, ((0, 0), (0, 0), (0, 0), (1, 0)))
    )
    gradient = render_grad + 2.0 * TV_WEIGHT * smooth
    square_sum = lax.psum(jnp.sum(gradient * gradient), ("slab", "tile"))
    norm_value = jnp.sqrt(square_sum)
    limit = CLIP_RMS * math.sqrt(4.0 * total_depth * total_x * rows_y)
    clipped = gradient * (limit / jnp.maximum(norm_value, limit))
    new_first = BETA_ONE * first_moment + (1.0 - BETA_ONE) * clipped
    new_second = BETA_TWO * second_moment + (1.0 - BETA_TWO) * clipped * clipped
    first_hat = new_first / (1.0 - BETA_ONE**STEP)
    second_hat = new_second / (1.0 - BETA_TWO**STEP)
    new_grid = voxel_grid - LEARN_RATE * first_hat / (jnp.sqrt(second_hat) + EPSILON)
    return (new_grid, new_first, new_second)


def solution(mesh):
    placed = (
        P(None, "slab", "tile", None),
        P(None, "slab", "tile", None),
        P(None, "slab", "tile", None),
        P("tile"),
        P("tile"),
        P("tile"),
        P(None, "tile"),
    )
    return jax.shard_map(
        per_device,
        mesh=mesh,
        in_specs=placed,
        out_specs=(
            P(None, "slab", "tile", None),
            P(None, "slab", "tile", None),
            P(None, "slab", "tile", None),
        ),
        check_vma=False,
    )
```

profile of v0, /device:TPU:0, one launch (start us, length us, event | category | flops | bytes accessed | tf_op | source)
XLA Modules:
  0.0 174.9 jit_solution(10069443243071050451)
XLA Ops:
  1.4 4.9 %collective-permute-start = (f32[4,1,8,256]{3,2,1,0:T(8,128)S(1)}, f32[4,1,8,256]{3,2,1,0:T(8,128)S(1)}, u32[]{:S(2)}, u32[]{:S(2)}) collective-permute-start(f32[4,1,8,256]{3,2,1,0:T(8,128)S(1)} %get-tuple-element.347), channel_id=1, source_target_pairs={{0,8},{8,16},{16,24},{1,9},{9,17},{17,25},{2,10},{10,18},{18,26},{... | collective-permute-start | bytes 98312 | tf_op jit(solution)/shard_map/ppermute | solution.py:31
  6.4 1.3 collective-permute-start.1
  9.6 30.4 %while.57 = (s32[]{:T(128)}, f32[4,64,1024]{2,1,0:T(8,128)S(1)}, f32[4,2048,1024]{2,1,0:T(8,128)}, s32[4,1024]{1,0:T(4,128)S(1)}, f32[64,2048]{1,0:T(8,128)S(1)}, /*index=5*/s32[]{:T(128)}) while((s32[]{:T(128)}, f32[4,64,1024]{2,1,0:T(8,128)S(1)}, f32[4,2048,1024]{2,1,0:T(8,128)}, s32[4,1024]{1,0:T(4,128)S(1)}, ...), condition=%wide.region_1.2_spmd.clone.clone, body=%wide.region_0.1_spmd.clone.clone.sunk | while | flops 1616904192 | bytes 9192013 | solution.py:96
  9.7 3.1 %fusion.69 = f32[4,64,1024]{2,1,0:T(8,128)S(1)} fusion(f32[4,64,1024]{2,1,0:T(8,128)S(1)} %get-tuple-element.495, s32[]{:T(128)} %get-tuple-element.494, f32[64,2048]{1,0:T(8,128)S(1)} %get-tuple-element.504, s32[1024]{0:T(1024)S(1)} %bitcast.79), kind=kOutput, calls=%fused_computation.12.clone.1 | convolution fusion | flops 1612709888 | bytes 790532 | tf_op jit(solution)/shard_map/jvp()/while/body/eval_jaxpr/dot_general | solution.py:92
  12.8 4.5 %convert_dynamic-update-slice_fusion.2 = f32[4,2048,1024]{2,1,0:T(8,128)} fusion(f32[4,2048,1024]{2,1,0:T(8,128)} %get-tuple-element.496, s32[]{:T(128)} %get-tuple-element.494, s32[1024]{0:T(1024)S(1)} %bitcast.80), kind=kLoop, calls=%fused_computation.8.clone.1 | loop fusion | flops 4194304 | bytes 8393216 | tf_op jit(solution)/shard_map/jvp()/while/body/jit(dynamic_update_index_in_dim)/dynamic_update_slice | solution.py:96
  17.3 3.1 %fusion.69 = f32[4,64,1024]{2,1,0:T(8,128)S(1)} fusion(f32[4,64,1024]{2,1,0:T(8,128)S(1)} %get-tuple-element.495, s32[]{:T(128)} %get-tuple-element.494, f32[64,2048]{1,0:T(8,128)S(1)} %get-tuple-element.504, s32[1024]{0:T(1024)S(1)} %bitcast.79), kind=kOutput, calls=%fused_computation.12.clone.1 | convolution fusion | flops 1612709888 | bytes 790532 | tf_op jit(solution)/shard_map/jvp()/while/body/eval_jaxpr/dot_general | solution.py:92
  20.4 4.5 %convert_dynamic-update-slice_fusion.2 = f32[4,2048,1024]{2,1,0:T(8,128)} fusion(f32[4,2048,1024]{2,1,0:T(8,128)} %get-tuple-element.496, s32[]{:T(128)} %get-tuple-element.494, s32[1024]{0:T(1024)S(1)} %bitcast.80), kind=kLoop, calls=%fused_computation.8.clone.1 | loop fusion | flops 4194304 | bytes 8393216 | tf_op jit(solution)/shard_map/jvp()/while/body/jit(dynamic_update_index_in_dim)/dynamic_update_slice | solution.py:96
  24.9 3.1 %fusion.69 = f32[4,64,1024]{2,1,0:T(8,128)S(1)} fusion(f32[4,64,1024]{2,1,0:T(8,128)S(1)} %get-tuple-element.495, s32[]{:T(128)} %get-tuple-element.494, f32[64,2048]{1,0:T(8,128)S(1)} %get-tuple-element.504, s32[1024]{0:T(1024)S(1)} %bitcast.79), kind=kOutput, calls=%fused_computation.12.clone.1 | convolution fusion | flops 1612709888 | bytes 790532 | tf_op jit(solution)/shard_map/jvp()/while/body/eval_jaxpr/dot_general | solution.py:92
  28.0 4.5 %convert_dynamic-update-slice_fusion.2 = f32[4,2048,1024]{2,1,0:T(8,128)} fusion(f32[4,2048,1024]{2,1,0:T(8,128)} %get-tuple-element.496, s32[]{:T(128)} %get-tuple-element.494, s32[1024]{0:T(1024)S(1)} %bitcast.80), kind=kLoop, calls=%fused_computation.8.clone.1 | loop fusion | flops 4194304 | bytes 8393216 | tf_op jit(solution)/shard_map/jvp()/while/body/jit(dynamic_update_index_in_dim)/dynamic_update_slice | solution.py:96
  32.5 3.1 %fusion.69 = f32[4,64,1024]{2,1,0:T(8,128)S(1)} fusion(f32[4,64,1024]{2,1,0:T(8,128)S(1)} %get-tuple-element.495, s32[]{:T(128)} %get-tuple-element.494, f32[64,2048]{1,0:T(8,128)S(1)} %get-tuple-element.504, s32[1024]{0:T(1024)S(1)} %bitcast.79), kind=kOutput, calls=%fused_computation.12.clone.1 | convolution fusion | flops 1612709888 | bytes 790532 | tf_op jit(solution)/shard_map/jvp()/while/body/eval_jaxpr/dot_general | solution.py:92
  35.6 4.5 %convert_dynamic-update-slice_fusion.2 = f32[4,2048,1024]{2,1,0:T(8,128)} fusion(f32[4,2048,1024]{2,1,0:T(8,128)} %get-tuple-element.496, s32[]{:T(128)} %get-tuple-element.494, s32[1024]{0:T(1024)S(1)} %bitcast.80), kind=kLoop, calls=%fused_computation.8.clone.1 | loop fusion | flops 4194304 | bytes 8393216 | tf_op jit(solution)/shard_map/jvp()/while/body/jit(dynamic_update_index_in_dim)/dynamic_update_slice | solution.py:96
  40.4 1.3 subtract_multiply_fusion.1
  46.0 15.2 %all-gather.1 = f32[4,3,4096]{2,1,0:T(4,128)S(1)} all-gather(f32[1,3,4096]{2,1,0:T(4,128)S(1)} %bitcast.77), channel_id=2, replica_groups=mesh['slab'=4,'tile'=8] {'slab'}, dimensions={0}, use_global_device_ids=true | all-gather | bytes 245760 | tf_op jit(solution)/shard_map/all_gather | solution.py:44
  61.2 13.1 %all-gather.2 = f32[4,1,4096]{2,1,0:T(1,128)S(1)} all-gather(f32[1,1,4096]{2,1,0:T(1,128)S(1)} %fusion.60), channel_id=1, replica_groups=mesh['slab'=4,'tile'=8] {'slab'}, dimensions={0}, use_global_device_ids=true | all-gather | bytes 81920 | tf_op jit(solution)/shard_map/all_gather | solution.py:44
  75.3 1.9 %fusion.19 = f32[1,16,4096]{2,1,0:T(8,128)S(1)} fusion(f32[16,4096]{1,0:T(8,128)S(1)} %bitcast.82, f32[1,4096]{1,0:T(1,128)S(1)} %bitcast.85, f32[16,4096]{1,0:T(8,128)S(1)} %get-tuple-element.343, s32[4096]{0:T(1024)S(1)} %get-tuple-element.349, s32[4096]{0:T(1024)S(1)} %get-tuple-element.348, s32[16]{0:T(128)S(1)} %iota_add_fusion.1, ...), kind=kOutput, calls=%fused_computation.25 | convolution fusion | flops 15859968 | bytes 1097792 | tf_op jit(solution)/shard_map/transpose(jvp())/dot_general | solution.py:99
  78.6 41.8 %while.58 = (s32[]{:T(128)}, f32[64,2048]{1,0:T(8,128)S(1)}, f32[4,64,1024]{2,1,0:T(8,128)S(1)}, f32[4,2048,1024]{2,1,0:T(8,128)}, s32[]{:T(128)}, /*index=5*/s32[]{:T(128)}, s32[]{:T(128)}) while((s32[]{:T(128)}, f32[64,2048]{1,0:T(8,128)S(1)}, f32[4,64,1024]{2,1,0:T(8,128)S(1)}, f32[4,2048,1024]{2,1,0:T(8,128)}, s32[]{:T(128)}, ...), condition=%wide.region_10.11_spmd.clone, body=%wide.region_9.10_spmd.clone.sunk | while | flops 1610874880 | bytes 9700962 | solution.py:96
  78.6 10.5 %fusion.72 = f32[64,2048]{1,0:T(8,128)S(1)} fusion(f32[4,2048,1024]{2,1,0:T(8,128)} %get-tuple-element.580, s32[]{:T(128)S(6)} %sub.139, f32[64,2048]{1,0:T(8,128)S(1)} %get-tuple-element.571, f32[4,64,1024]{2,1,0:T(8,128)S(1)} %get-tuple-element.579, pred[]{:T(512)S(6)} %compare.8), kind=kOutput, calls=%fused_computation.17.clone.1 | convolution fusion | flops 1610874880 | bytes 9700864 | tf_op jit(solution)/shard_map/transpose(jvp())/while/body/eval_jaxpr/dot_general | solution.py:92
  89.1 10.4 %fusion.72 = f32[64,2048]{1,0:T(8,128)S(1)} fusion(f32[4,2048,1024]{2,1,0:T(8,128)} %get-tuple-element.580, s32[]{:T(128)S(6)} %sub.139, f32[64,2048]{1,0:T(8,128)S(1)} %get-tuple-element.571, f32[4,64,1024]{2,1,0:T(8,128)S(1)} %get-tuple-element.579, pred[]{:T(512)S(6)} %compare.8), kind=kOutput, calls=%fused_computation.17.clone.1 | convolution fusion | flops 1610874880 | bytes 9700864 | tf_op jit(solution)/shard_map/transpose(jvp())/while/body/eval_jaxpr/dot_general | solution.py:92
  99.5 10.4 %fusion.72 = f32[64,2048]{1,0:T(8,128)S(1)} fusion(f32[4,2048,1024]{2,1,0:T(8,128)} %get-tuple-element.580, s32[]{:T(128)S(6)} %sub.139, f32[64,2048]{1,0:T(8,128)S(1)} %get-tuple-element.571, f32[4,64,1024]{2,1,0:T(8,128)S(1)} %get-tuple-element.579, pred[]{:T(512)S(6)} %compare.8), kind=kOutput, calls=%fused_computation.17.clone.1 | convolution fusion | flops 1610874880 | bytes 9700864 | tf_op jit(solution)/shard_map/transpose(jvp())/while/body/eval_jaxpr/dot_general | solution.py:92
  109.9 10.4 %fusion.72 = f32[64,2048]{1,0:T(8,128)S(1)} fusion(f32[4,2048,1024]{2,1,0:T(8,128)} %get-tuple-element.580, s32[]{:T(128)S(6)} %sub.139, f32[64,2048]{1,0:T(8,128)S(1)} %get-tuple-element.571, f32[4,64,1024]{2,1,0:T(8,128)S(1)} %get-tuple-element.579, pred[]{:T(512)S(6)} %compare.8), kind=kOutput, calls=%fused_computation.17.clone.1 | convolution fusion | flops 1610874880 | bytes 9700864 | tf_op jit(solution)/shard_map/transpose(jvp())/while/body/eval_jaxpr/dot_general | solution.py:92
  120.8 1.3 collective-permute-start.2
  123.5 3.4 %collective-permute-done.3 = f32[4,18,1,256]{3,1,2,0:T(8,128)S(1)} collective-permute-done((f32[4,18,1,256]{3,1,2,0:T(8,128)S(1)}, f32[4,18,1,256]{3,1,2,0:T(8,128)S(1)}, u32[]{:S(2)}, u32[]{:S(2)}) %collective-permute-start.3) | collective-permute-done | bytes 73760 | tf_op jit(solution)/shard_map/ppermute | solution.py:33
  128.2 43.4 %psum.7 = f32[]{:T(128)} all-reduce(f32[]{:T(128)} %get-tuple-element.336), channel_id=1, replica_groups=mesh['slab'=4,'tile'=8] {'slab','tile'}, use_global_device_ids=true, to_apply=%region_12.13 | all-reduce | flops 1 | bytes 8 | tf_op jit(solution)/shard_map/psum | solution.py:133
  172.4 2.5 %divide_subtract_fusion = (f32[4,16,8,256]{3,2,1,0:T(8,128)}, f32[4,16,8,256]{3,2,1,0:T(8,128)}, f32[4,16,8,256]{3,2,1,0:T(8,128)}) fusion(f32[4,16,8,256]{3,2,1,0:T(8,128)S(1)} %copy-done, f32[4,16,8,256]{3,2,1,0:T(8,128)S(1)} %get-tuple-element.337, f32[]{:T(128)S(6)} %div.22, f32[4,16,8,256]{3,2,1,0:T(8,128)} %param.16, f32[4,16,8,256]{3,2,1,0:T(8,128)} %param.17), kind=kLoop, calls=%fused_computation.60 | loop fusion | flops 1703936 | bytes 3670020 | tf_op jit(solution)/shard_map/sub | solution.py:141
  (73 shorter events, 12.7 us)
Async XLA Ops:
  1.4 119.1 %collective-permute-start = (f32[4,1,8,256]{3,2,1,0:T(8,128)S(1)}, f32[4,1,8,256]{3,2,1,0:T(8,128)S(1)}, u32[]{:S(2)}, u32[]{:S(2)}) collective-permute-start(f32[4,1,8,256]{3,2,1,0:T(8,128)S(1)} %get-tuple-element.347), channel_id=1, source_target_pairs={{0,8},{8,16},{16,24},{1,9},{9,17},{17,25},{2,10},{10,18},{18,26},{... | collective-permute-start | bytes 98312 | tf_op jit(solution)/shard_map/ppermute | solution.py:31
  6.4 114.3 %collective-permute-start.1 = (f32[4,1,8,256]{3,2,1,0:T(8,128)S(1)}, f32[4,1,8,256]{3,2,1,0:T(8,128)S(1)}, u32[]{:S(2)}, u32[]{:S(2)}) collective-permute-start(f32[4,1,8,256]{3,2,1,0:T(8,128)S(1)} %get-tuple-element.346), channel_id=1, source_target_pairs={{8,0},{16,8},{24,16},{9,1},{17,9},{25,17},{10,2},{18,10},{26,18},{... | collective-permute-start | bytes 98312 | tf_op jit(solution)/shard_map/ppermute | solution.py:33
  9.6 30.7 %copy-start.4 = (s32[4096]{0:T(1024)S(1)}, s32[4096]{0:T(1024)}, u32[]{:S(2)}) copy-start(s32[4096]{0:T(1024)} %param.19) | copy-start | bytes 49156
  9.6 30.7 %copy-start.5 = (s32[4096]{0:T(1024)S(1)}, s32[4096]{0:T(1024)}, u32[]{:S(2)}) copy-start(s32[4096]{0:T(1024)} %param.20) | copy-start | bytes 49156
  9.6 33.9 %copy-start = (f32[4,16,8,256]{3,2,1,0:T(8,128)S(1)}, f32[4,16,8,256]{3,2,1,0:T(8,128)}, u32[]{:S(2)}) copy-start(f32[4,16,8,256]{3,2,1,0:T(8,128)} %param.15) | copy-start | bytes 1572868
  40.1 34.9 %copy-start.3 = (f32[3,4096]{1,0:T(4,128)S(1)}, f32[3,4096]{1,0:T(4,128)}, u32[]{:S(2)}) copy-start(f32[3,4096]{1,0:T(4,128)} %param.21) | copy-start | bytes 147460
  78.6 48.5 %copy-start.1 = (f32[4,16,8,255]{3,2,1,0:T(8,128)S(1)}, f32[4,16,8,255]{3,2,1,0:T(8,128)}, u32[]{:S(2)}) copy-start(f32[4,16,8,255]{3,2,1,0:T(8,128)} %get-tuple-element.338) | copy-start | bytes 1566724
  78.6 48.5 %copy-start.2 = (f32[4,16,8,255]{3,2,1,0:T(8,128)S(1)}, f32[4,16,8,255]{3,2,1,0:T(8,128)}, u32[]{:S(2)}) copy-start(f32[4,16,8,255]{3,2,1,0:T(8,128)} %get-tuple-element.339) | copy-start | bytes 1566724
  120.8 2.6 %collective-permute-start.2 = (f32[4,18,1,256]{3,1,2,0:T(8,128)S(1)}, f32[4,18,1,256]{3,1,2,0:T(8,128)S(1)}, u32[]{:S(2)}, u32[]{:S(2)}) collective-permute-start(f32[4,18,1,256]{3,1,2,0:T(8,128)S(1)} %copy.39), channel_id=1, source_target_pairs={{0,1},{1,2},{2,3},{3,4},{4,5},{5,6},{6,7},{8,9},{9,10},{10,11},{11... | collective-permute-start | bytes 221192 | tf_op jit(solution)/shard_map/ppermute | solution.py:31
  122.1 4.9 %collective-permute-start.3 = (f32[4,18,1,256]{3,1,2,0:T(8,128)S(1)}, f32[4,18,1,256]{3,1,2,0:T(8,128)S(1)}, u32[]{:S(2)}, u32[]{:S(2)}) collective-permute-start(f32[4,18,1,256]{3,1,2,0:T(8,128)S(1)} %copy.41), channel_id=1, source_target_pairs={{1,0},{2,1},{3,2},{4,3},{5,4},{6,5},{7,6},{9,8},{10,9},{11,10},{12... | collective-permute-start | bytes 221192 | tf_op jit(solution)/shard_map/ppermute | solution.py:33
where the time goes:
time: 175 us
  blocking collectives  71.7 us (41%)
  matrix products  57.4 us (33%)
  other arithmetic  25.5 us (15%)
  starting transfers between devices  8.83 us (5%)
  local copies, waits for them, and re-layouts  5.79 us (3%)
  waiting for transfers between devices  3.45 us (2%)
  between operations  1.79 us (1%)
    dot_general x8, matrix products, pick_block(): jnp.dot(flat, selector, precision=lax.Precision.HIGHEST, preferred_elemen...  54.2 us
    psum x1, blocking collectives, per_device(): square_sum = lax.psum(jnp.sum(gradient * gradient), ('slab', 'tile'))  43.4 us
    all_gather x2, blocking collectives, carried_in(): gathered = jax.tree.map(lambda a: lax.all_gather(a, axis), part)  28.3 us
    dynamic_update_slice x4, other arithmetic, march_slab(): picked = lax.map(pick_block, pixel_blocks)  17.8 us
    ppermute x2, starting transfers between devices, padded_2(): lax.ppermute(tail, axis, [(i, (i + 1) % count) for i in range(ends)])  6.24 us
  transfers between devices with their start and end apart: 4, of which 1 were waited for; matrix products, arithmetic and copies ran while one was open for 48% of the time, Pallas kernels for 0%

commit v1 on v0

v1 whole, which is shorter than its diff:
```python
import math

import jax
import jax.numpy as jnp
from jax import lax
from jax.experimental import pallas as pl
from jax.experimental.pallas import tpu as pltpu
from jax.sharding import PartitionSpec as P

STEP = 20


RENDER_WEIGHT = 1000.0
TV_WEIGHT = 0.05
BACKGROUND = 1.0
STEP_SPAN = 4.0
CLIP_RMS = 0.25
LEARN_RATE = 0.02
BETA_ONE = 0.9
BETA_TWO = 0.99
EPSILON = 1e-08
BLOCK_LIMIT = 1024


def split_bf16(value):
    high = value.astype(jnp.bfloat16)
    low = (value - high.astype(jnp.float32)).astype(jnp.bfloat16)
    return high, low


def softplus(value):
    return jnp.maximum(value, 0.0) + jnp.log1p(jnp.exp(-jnp.abs(value)))


def ray_keys(pixel, start, count, slab_pos, depth, rows_x, rows_y):
    shift = rows_y.bit_length() - 1
    x = jnp.right_shift(pixel, shift)
    y = jnp.bitwise_and(pixel, rows_y - 1)
    first = (start - slab_pos) * depth
    used = jnp.clip(first + count, 0, depth)
    key = jnp.where((first <= 0) & (used > 0), (used - 1) * rows_x + x, -1)
    return y, key


def one_hot(y, rows_y):
    ids = lax.broadcasted_iota(jnp.int32, (rows_y, y.shape[1]), 0)
    return jnp.where(ids == y, 1.0, 0.0).astype(jnp.bfloat16)


def forward_kernel(total_depth, grid, pixel, start, count, part, to_next, to_prev, table):
    channels, depth, rows_x, rows_y = grid.shape
    rows = depth * rows_x
    rays = pixel.shape[1]
    half = rays // 2
    slab_pos = lax.axis_index("slab")
    reach = jnp.ones((rows_x, rows_y), jnp.float32)
    sums = [jnp.zeros((rows_x, rows_y), jnp.float32) for _ in range(3)]
    held = []
    for z in range(depth):
        fade = jnp.exp(-softplus(grid[0, z]) * (STEP_SPAN / total_depth))
        weight = reach * (1.0 - fade)
        reach = reach * fade
        sums = [sums[c] + weight * lax.logistic(grid[c + 1, z]) for c in range(3)]
        held.append(sums + [reach])
        if z % 2:
            for c in range(4):
                high, low = split_bf16(jnp.concatenate([held[0][c], held[1][c]], axis=0))
                at = c * rows + (z - 1) * rows_x
                table[at : at + 2 * rows_x, :rows_y] = high
                table[at : at + 2 * rows_x, rows_y:] = low
            held = []
    block = math.gcd(half, 512)
    for at in range(0, rays, block):
        where = slice(at, at + block)
        y, key = ray_keys(
            pixel[:, where], start[:, where], count[:, where], slab_pos, depth, rows_x, rows_y
        )
        hot = one_hot(y, rows_y)
        picked = jnp.dot(
            table[...], jnp.concatenate([hot, hot], axis=0), preferred_element_type=jnp.float32
        )
        match = lax.broadcasted_iota(jnp.int32, (rows, block), 0) == key
        found = [
            jnp.sum(
                jnp.where(match, picked[c * rows : (c + 1) * rows], 0.0), axis=0, keepdims=True
            )
            for c in range(4)
        ]
        found[3] = jnp.where(key < 0, 1.0, found[3])
        found = jnp.concatenate(found, axis=0)
        row = 4 * (at // half)
        lane = at % half
        for out in (part, to_next, to_prev):
            out[row : row + 4, lane : lane + block] = found
    for c in range(channels):
        at = half + c * rows_y
        to_next[:, at : at + rows_y] = grid[c, depth - 1]
        to_prev[:, at : at + rows_y] = grid[c, 0]


def backward_kernel(
    slab_count, tile_count, grid, pixel, start, count, target, x_low, x_high, part, *rest
):
    others = rest[: slab_count - 1]
    gradient, square, left, right, spread = rest[slab_count - 1 :]
    channels, depth, rows_x, rows_y = grid.shape
    rows = depth * rows_x
    rays = pixel.shape[1]
    half = rays // 2
    total_depth = depth * slab_count
    slab_pos = lax.axis_index("slab")
    tile_pos = lax.axis_index("tile")
    block = math.gcd(half, 1024)
    for at in range(0, rays, block):
        where = slice(at, at + block)
        row = 4 * (at // half)
        lanes = slice(at % half, at % half + block)

        def piece(ref):
            return ref[row : row + 3, lanes], ref[row + 3 : row + 4, lanes]

        front_color = jnp.zeros((3, block), jnp.float32)
        front_trans = jnp.ones((1, block), jnp.float32)
        beyond = jnp.full((3, block), BACKGROUND, jnp.float32)
        for k in range(slab_count - 1, 0, -1):
            color, trans = piece(others[k - 1])
            nearer = slab_pos >= k
            front_color = jnp.where(nearer, front_color + front_trans * color, front_color)
            front_trans = jnp.where(nearer, front_trans * trans, front_trans)
            color, trans = piece(others[slab_count - k - 1])
            farther = slab_pos + k < slab_count
            beyond = jnp.where(farther, color + trans * beyond, beyond)
        own_color, own_trans = piece(part)
        rendered = front_color + front_trans * (own_color + own_trans * beyond)
        residual = RENDER_WEIGHT * (rendered - target[:, where])
        color_cot = front_trans * residual
        trans_cot = front_trans * jnp.sum(residual * beyond, axis=0, keepdims=True)
        y, key = ray_keys(
            pixel[:, where], start[:, where], count[:, where], slab_pos, depth, rows_x, rows_y
        )
        hot = one_hot(y, rows_y)
        match = lax.broadcasted_iota(jnp.int32, (rows, block), 0) == key
        for c in range(4):
            cot = color_cot[c : c + 1] if c < 3 else trans_cot
            high = cot.astype(jnp.bfloat16).astype(jnp.float32)
            low = cot - high
            for j, value in enumerate((high, low)):
                left[c * rows : (c + 1) * rows, j * block : (j + 1) * block] = jnp.where(
                    match, value, 0.0
                ).astype(jnp.bfloat16)
        for j in range(2):
            right[:, j * block : (j + 1) * block] = hot
        added = lax.dot_general(
            left[...], right[...], (((1,), (1,)), ((), ())), preferred_element_type=jnp.float32
        )
        if at == 0:
            spread[...] = added
        else:
            spread[...] += added

    reach = [jnp.ones((rows_x, rows_y), jnp.float32)]
    fades = []
    for z in range(depth):
        fades.append(jnp.exp(-softplus(grid[0, z]) * (STEP_SPAN / total_depth)))
        reach.append(reach[z] * fades[z])
    row_ids = lax.broadcasted_iota(jnp.int32, (rows_x, rows_y), 0)
    lane_ids = lax.broadcasted_iota(jnp.int32, (rows_x, rows_y), 1)
    has_low = (row_ids > 0) | (tile_pos > 0)
    has_high = (row_ids < rows_x - 1) | (tile_pos < tile_count - 1)
    total = jnp.zeros((rows_x, rows_y), jnp.float32)

    def smooth(c, z):
        value = grid[c, z]
        lanes = slice(half + c * rows_y, half + (c + 1) * rows_y)
        if z > 0:
            out = value - grid[c, z - 1]
        else:
            out = jnp.where(slab_pos > 0, value - others[0][:, lanes], 0.0)
        if z < depth - 1:
            out = out + (value - grid[c, z + 1])
        else:
            out = out + jnp.where(
                slab_pos < slab_count - 1, value - others[slab_count - 2][:, lanes], 0.0
            )
        at = c * depth + z
        low = jnp.where(row_ids == 0, x_low[at : at + 1], pltpu.roll(value, 1, 0))
        high = jnp.where(
            row_ids == rows_x - 1, x_high[at : at + 1], pltpu.roll(value, rows_x - 1, 0)
        )
        out = out + jnp.where(has_low, value - low, 0.0) + jnp.where(has_high, value - high, 0.0)
        out = out + jnp.where(lane_ids > 0, value - pltpu.roll(value, 1, 1), 0.0)
        out = out + jnp.where(
            lane_ids < rows_y - 1, value - pltpu.roll(value, rows_y - 1, 1), 0.0
        )
        return (2.0 * TV_WEIGHT) * out

    below = [jnp.zeros((rows_x, rows_y), jnp.float32) for _ in range(3)]
    gain_after = jnp.zeros((rows_x, rows_y), jnp.float32)
    tail = jnp.zeros((rows_x, rows_y), jnp.float32)
    for z in range(depth - 1, -1, -1):
        rate = 1.0 - fades[z]
        weight = reach[z] * rate
        gain = jnp.zeros((rows_x, rows_y), jnp.float32)
        for c in range(3):
            at = c * rows + z * rows_x
            below[c] = below[c] + spread[at : at + rows_x]
            shade = lax.logistic(grid[c + 1, z])
            gain = gain + shade * below[c]
            value = weight * below[c] * shade * (1.0 - shade) + smooth(c + 1, z)
            gradient[c + 1, z] = value
            total = total + value * value
        at = 3 * rows + z * rows_x
        tail = tail + reach[z + 1] * (gain_after - gain + spread[at : at + rows_x])
        value = smooth(0, z) - tail * (STEP_SPAN / total_depth) * lax.logistic(grid[0, z])
        gradient[0, z] = value
        total = total + value * value
        gain_after = gain
    square[...] = jnp.broadcast_to(jnp.sum(total).reshape(1, 1), square.shape)


def group_sum(value, axis, masks):
    count = lax.axis_size(axis)
    parts = [lax.ppermute(value, axis, [(i, i ^ m) for i in range(count)]) for m in masks]
    for part in parts:
        value = value + part
    return value


def global_sum(value):
    for axis in ("slab", "tile"):
        left = lax.axis_size(axis)
        base = 1
        rounds = []
        if axis == "tile":
            rounds.append([1])
            base = 2
        while base < left:
            if base * 4 <= left:
                rounds.append([base, 2 * base, 3 * base])
                base *= 4
            else:
                rounds.append([base])
                base *= 2
        for masks in reversed(rounds):
            value = group_sum(value, axis, masks)
    return value


def per_device(voxel_grid, first_moment, second_moment, pixel_index, start_slab, ray_count, target):
    slab_count = lax.axis_size("slab")
    tile_count = lax.axis_size("tile")
    channels, depth, rows_x, rows_y = voxel_grid.shape
    total_depth = depth * slab_count
    total_x = rows_x * tile_count
    rays = pixel_index.shape[0]
    half = rays // 2
    f32 = jnp.float32
    pixel = pixel_index.reshape(1, rays)
    start = start_slab.reshape(1, rays)
    count = ray_count.reshape(1, rays)
    first_rows = voxel_grid[:, :, 0, :].reshape(channels * depth, rows_y)
    last_rows = voxel_grid[:, :, rows_x - 1, :].reshape(channels * depth, rows_y)
    x_low = lax.ppermute(last_rows, "tile", [(i, i + 1) for i in range(tile_count - 1)])
    x_high = lax.ppermute(first_rows, "tile", [(i + 1, i) for i in range(tile_count - 1)])
    wide = jax.ShapeDtypeStruct((8, half + channels * rows_y), f32)
    part, to_next, to_prev = pl.pallas_call(
        lambda *refs: forward_kernel(total_depth, *refs),
        out_shape=(jax.ShapeDtypeStruct((8, half), f32), wide, wide),
        scratch_shapes=[pltpu.VMEM((4 * depth * rows_x, 2 * rows_y), jnp.bfloat16)],
        name="forward",
    )(voxel_grid, pixel, start, count)
    others = []
    for k in range(1, slab_count):
        sent = to_next if k == 1 else to_prev if k == slab_count - 1 else part
        others.append(
            lax.ppermute(sent, "slab", [(i, (i + k) % slab_count) for i in range(slab_count)])
        )
    block = math.gcd(half, 1024)
    gradient, square = pl.pallas_call(
        lambda *refs: backward_kernel(slab_count, tile_count, *refs),
        out_shape=(
            jax.ShapeDtypeStruct(voxel_grid.shape, f32),
            jax.ShapeDtypeStruct((1, 128), f32),
        ),
        scratch_shapes=[
            pltpu.VMEM((4 * depth * rows_x, 2 * block), jnp.bfloat16),
            pltpu.VMEM((rows_y, 2 * block), jnp.bfloat16),
            pltpu.VMEM((4 * depth * rows_x, rows_y), f32),
        ],
        name="backward",
    )(voxel_grid, pixel, start, count, target, x_low, x_high, part, *others)
    square_sum = global_sum(square)[0, 0]
    norm_value = jnp.sqrt(square_sum)
    limit = CLIP_RMS * math.sqrt(4.0 * total_depth * total_x * rows_y)
    clipped = gradient * (limit / jnp.maximum(norm_value, limit))
    new_first = BETA_ONE * first_moment + (1.0 - BETA_ONE) * clipped
    new_second = BETA_TWO * second_moment + (1.0 - BETA_TWO) * clipped * clipped
    first_hat = new_first / (1.0 - BETA_ONE**STEP)
    second_hat = new_second / (1.0 - BETA_TWO**STEP)
    new_grid = voxel_grid - LEARN_RATE * first_hat / (jnp.sqrt(second_hat) + EPSILON)
    return (new_grid, new_first, new_second)


def solution(mesh):
    placed = (
        P(None, "slab", "tile", None),
        P(None, "slab", "tile", None),
        P(None, "slab", "tile", None),
        P("tile"),
        P("tile"),
        P("tile"),
        P(None, "tile"),
    )
    return jax.shard_map(
        per_device,
        mesh=mesh,
        in_specs=placed,
        out_specs=(
            P(None, "slab", "tile", None),
            P(None, "slab", "tile", None),
            P(None, "slab", "tile", None),
        ),
        check_vma=False,
    )
```

time: 175 us -> 47.7 us (0.27)
  blocking collectives: 71.7 us -> 0 us
  matrix products: 57.4 us -> 0 us
  other arithmetic: 25.5 us -> 2.4 us
  starting transfers between devices: 8.83 us -> 20.1 us
  Pallas kernels: 0 us -> 9.69 us
  waiting for transfers between devices: 3.45 us -> 11.2 us
  local copies, waits for them, and re-layouts: 5.79 us -> 3.27 us
    dot_general x10 -> x0, matrix products: 57.4 us -> none  [the longest x8 54.2 us: pick_block(): jnp.dot(flat, selector, precision=lax.Precision.HIGHEST, preferred_elemen...]
    psum x1 -> x0, blocking collectives: 43.4 us -> none  [per_device(): square_sum = lax.psum(jnp.sum(gradient * gradient), ('slab', 'tile'))]
    all_gather x2 -> x0, blocking collectives: 28.3 us -> none  [carried_in(): gathered = jax.tree.map(lambda a: lax.all_gather(a, axis), part)]
    dynamic_update_slice x4 -> x0, other arithmetic: 17.8 us -> none  [march_slab(): picked = lax.map(pick_block, pixel_blocks)]
    ppermute x4 -> x12, starting transfers between devices: 8.83 us -> 20.1 us  [the longest x7 11.3 us: group_sum(): lax.ppermute(value, axis, [(i, i ^ m) for i in range(count)])]
    pallas_call x0 -> x2, Pallas kernels: none -> 9.69 us  [the longest x1 5.09 us: per_device(): pl.pallas_call(lambda *refs: backward_kernel(slab_count, tile_count, *ref...]
    ppermute x4 -> x12, waiting for transfers between devices: 3.45 us -> 11.2 us  [the longest x7 6.62 us: group_sum(): lax.ppermute(value, axis, [(i, i ^ m) for i in range(count)])]
    reshape x3 -> x0, local copies, waits for them, and re-layouts: 2.05 us -> none  [the longest x2 1.32 us: march_slab(): samples = picked.transpose(1, 0, 2).reshape(channels, slab_depth, ray_total)]
  transfers between devices with their start and end apart: 4 -> 12, of which waited for: 1 -> 8; matrix products, arithmetic and copies ran while one was open for 48% -> 3% of each run, Pallas kernels for 0% -> 0%
where the time goes in v1:
time: 47.7 us; the launch traced here: 47.5 us
  starting transfers between devices  20.1 us (42%)
  waiting for transfers between devices  11.2 us (23%)
  Pallas kernels  9.69 us (20%)
  local copies, waits for them, and re-layouts  3.27 us (7%)
  other arithmetic  2.4 us (5%)
  between operations  0.87 us (2%)
    ppermute x7, starting transfers between devices, group_sum(): lax.ppermute(value, axis, [(i, i ^ m) for i in range(count)])  11.3 us
    ppermute x7, waiting for transfers between devices, group_sum(): lax.ppermute(value, axis, [(i, i ^ m) for i in range(count)])  6.62 us
    ppermute x3, starting transfers between devices, per_device(): lax.ppermute(sent, 'slab', [(i, (i + k) % slab_count) for i in range(slab...  5.99 us
    pallas_call x1, Pallas kernels, per_device(): pl.pallas_call(lambda *refs: backward_kernel(slab_count, tile_count, *ref...  5.09 us
    pallas_call x1, Pallas kernels, per_device(): pl.pallas_call(lambda *refs: forward_kernel(total_depth, *refs), out_shap...  4.6 us
    ppermute x1, waiting for transfers between devices, per_device(): lax.ppermute(first_rows, 'tile', [(i + 1, i) for i in range(tile_count -...  2.69 us
    sub x1, other arithmetic, per_device(): voxel_grid - LEARN_RATE * first_hat / (jnp.sqrt(second_hat) + EPSILON)  2.39 us
    unnamed x20, local copies, waits for them, and re-layouts  1.92 us
  transfers between devices with their start and end apart: 12, of which 8 were waited for; matrix products, arithmetic and copies ran while one was open for 3% of the time, Pallas kernels for 0%

profile of v1, /device:TPU:0, one launch (start us, length us, event | category | flops | bytes accessed | tf_op | source)
XLA Modules:
  0.0 47.5 jit_solution(6675721259093527961)
XLA Ops:
  0.6 4.6 %forward.1 = (f32[8,2048]{1,0:T(8,128)}, f32[8,3072]{1,0:T(8,128)}, f32[8,3072]{1,0:T(8,128)}) custom-call(f32[4,16,8,256]{3,2,1,0:T(8,128)} %refs_0_.3, s32[1,4096]{1,0:T(1,128)} %bitcast.7, s32[1,4096]{1,0:T(1,128)} %bitcast.9, s32[1,4096]{1,0:T(1,128)} %bitcast.11), custom_call_target="tpu_custom_call" | custom-call | tf_op jit(solution)/shard_map/forward/pallas_call | solution.py:266
  5.2 3.1 %collective-permute-start.2 = (f32[8,3072]{1,0:T(8,128)}, f32[8,3072]{1,0:T(8,128)S(1)}, u32[]{:S(2)}, u32[]{:S(2)}) collective-permute-start(f32[8,3072]{1,0:T(8,128)} %get-tuple-element.9), channel_id=1, source_target_pairs={{0,8},{8,16},{16,24},{24,0},{1,9},{9,17},{17,25},{25,1},{2,10},{10... | collective-permute-start | bytes 294920 | tf_op jit(solution)/shard_map/ppermute | solution.py:276
  8.3 2.0 %collective-permute-start.4 = (f32[8,3072]{1,0:T(8,128)}, f32[8,3072]{1,0:T(8,128)S(1)}, u32[]{:S(2)}, u32[]{:S(2)}) collective-permute-start(f32[8,3072]{1,0:T(8,128)} %get-tuple-element.10), channel_id=1, source_target_pairs={{0,24},{8,0},{16,8},{24,16},{1,25},{9,1},{17,9},{25,17},{2,26},{10... | collective-permute-start | bytes 294920 | tf_op jit(solution)/shard_map/ppermute | solution.py:276
  10.3 1.4 %fusion.2 = (f32[4,16,1,256]{3,2,1,0:T(1,128)S(1)}, f32[4,16,1,256]{3,2,1,0:T(1,128)S(1)}) fusion(f32[4,16,8,256]{3,2,1,0:T(8,128)} %refs_0_.3), kind=kLoop, calls=%fused_computation.6 | loop fusion | bytes 262144 | tf_op jit(solution)/shard_map/slice | solution.py:261
  11.7 1.5 %collective-permute-start = (f32[64,256]{1,0:T(8,128)S(1)}, f32[64,256]{1,0:T(8,128)S(1)}, u32[]{:S(2)}, u32[]{:S(2)}) collective-permute-start(f32[64,256]{1,0:T(8,128)S(1)} %bitcast.13), channel_id=1, source_target_pairs={{0,1},{1,2},{2,3},{3,4},{4,5},{5,6},{6,7},{8,9},{9,10},{10,11},{11... | collective-permute-start | bytes 196616 | tf_op jit(solution)/shard_map/ppermute | solution.py:263
  13.2 1.3 %collective-permute-start.1 = (f32[64,256]{1,0:T(8,128)S(1)}, f32[64,256]{1,0:T(8,128)S(1)}, u32[]{:S(2)}, u32[]{:S(2)}) collective-permute-start(f32[64,256]{1,0:T(8,128)S(1)} %bitcast.14), channel_id=1, source_target_pairs={{1,0},{2,1},{3,2},{4,3},{5,4},{6,5},{7,6},{9,8},{10,9},{11,10},{12... | collective-permute-start | bytes 196616 | tf_op jit(solution)/shard_map/ppermute | solution.py:264
  14.5 0.9 %collective-permute-start.3 = (f32[8,2048]{1,0:T(8,128)}, f32[8,2048]{1,0:T(8,128)S(1)}, u32[]{:S(2)}, u32[]{:S(2)}) collective-permute-start(f32[8,2048]{1,0:T(8,128)} %get-tuple-element.8.refs_7_), channel_id=1, source_target_pairs={{0,16},{8,24},{16,0},{24,8},{1,17},{9,25},{17,1},{25,9},{2,18},{10... | collective-permute-start | bytes 196616 | tf_op jit(solution)/shard_map/ppermute | solution.py:276
  15.4 2.7 %collective-permute-done.1.refs_6_ = f32[64,256]{1,0:T(8,128)S(1)} collective-permute-done((f32[64,256]{1,0:T(8,128)S(1)}, f32[64,256]{1,0:T(8,128)S(1)}, u32[]{:S(2)}, u32[]{:S(2)}) %collective-permute-start.1) | collective-permute-done | bytes 65568 | tf_op jit(solution)/shard_map/ppermute | solution.py:264
  18.1 1.8 %collective-permute-done.3.refs_9_ = f32[8,2048]{1,0:T(8,128)S(1)} collective-permute-done((f32[8,2048]{1,0:T(8,128)}, f32[8,2048]{1,0:T(8,128)S(1)}, u32[]{:S(2)}, u32[]{:S(2)}) %collective-permute-start.3) | collective-permute-done | bytes 65568 | tf_op jit(solution)/shard_map/ppermute | solution.py:276
  20.0 0.6 %copy-done.7 = f32[8,2048]{1,0:T(8,128)} copy-done((f32[8,2048]{1,0:T(8,128)}, f32[8,2048]{1,0:T(8,128)S(1)}, u32[]{:S(2)}) %copy-start.7) | copy-done | bytes 65560
  20.6 0.6 %copy-done.4 = f32[8,3072]{1,0:T(8,128)} copy-done((f32[8,3072]{1,0:T(8,128)}, f32[8,3072]{1,0:T(8,128)S(1)}, u32[]{:S(2)}) %copy-start.4) | copy-done | bytes 98328
  21.2 5.1 %backward.1 = (f32[4,16,8,256]{3,2,1,0:T(8,128)}, f32[1,128]{1,0:T(1,128)}) custom-call(f32[4,16,8,256]{3,2,1,0:T(8,128)} %refs_0_.3, s32[1,4096]{1,0:T(1,128)} %bitcast.8, s32[1,4096]{1,0:T(1,128)} %bitcast.10, s32[1,4096]{1,0:T(1,128)} %bitcast.12, f32[3,4096]{1,0:T(4,128)} %refs_4_.1, f32[64,256]{1,0:T(8,128)} %copy-done.5, f32[64,256]{1,0:T(8,128)} %copy-done.6, ...), custom_call_target="tpu_custom_call" | custom-call | tf_op jit(solution)/shard_map/backward/pallas_call | solution.py:279
  26.3 0.6 %copy-done.8 = f32[1,128]{1,0:T(1,128)S(1)} copy-done((f32[1,128]{1,0:T(1,128)S(1)}, f32[1,128]{1,0:T(1,128)}, u32[]{:S(2)}) %copy-start.8) | copy-done | bytes 536
  26.9 2.4 %collective-permute-start.7 = (f32[1,128]{1,0:T(1,128)S(1)}, f32[1,128]{1,0:T(1,128)S(1)}, u32[]{:S(2)}, u32[]{:S(2)}) collective-permute-start(f32[1,128]{1,0:T(1,128)S(1)} %copy-done.8), channel_id=1, source_target_pairs={{0,24},{8,16},{16,8},{24,0},{1,25},{9,17},{17,9},{25,1},{2,26},{10... | collective-permute-start | bytes 1544 | tf_op jit(solution)/shard_map/ppermute | solution.py:223
  29.4 1.9 %collective-permute-start.5 = (f32[1,128]{1,0:T(1,128)S(1)}, f32[1,128]{1,0:T(1,128)S(1)}, u32[]{:S(2)}, u32[]{:S(2)}) collective-permute-start(f32[1,128]{1,0:T(1,128)S(1)} %copy-done.8), channel_id=1, source_target_pairs={{0,8},{8,0},{16,24},{24,16},{1,9},{9,1},{17,25},{25,17},{2,10},{10... | collective-permute-start | bytes 1544 | tf_op jit(solution)/shard_map/ppermute | solution.py:223
  31.3 1.0 %collective-permute-done.7 = f32[1,128]{1,0:T(1,128)S(1)} collective-permute-done((f32[1,128]{1,0:T(1,128)S(1)}, f32[1,128]{1,0:T(1,128)S(1)}, u32[]{:S(2)}, u32[]{:S(2)}) %collective-permute-start.7) | collective-permute-done | bytes 544 | tf_op jit(solution)/shard_map/ppermute | solution.py:223
  32.3 1.5 %collective-permute-done.6 = f32[1,128]{1,0:T(1,128)S(1)} collective-permute-done((f32[1,128]{1,0:T(1,128)S(1)}, f32[1,128]{1,0:T(1,128)S(1)}, u32[]{:S(2)}, u32[]{:S(2)}) %collective-permute-start.6) | collective-permute-done | bytes 544 | tf_op jit(solution)/shard_map/ppermute | solution.py:223
  33.9 5.5 %collective-permute-start.10 = (f32[1,128]{1,0:T(1,128)S(1)}, f32[1,128]{1,0:T(1,128)S(1)}, u32[]{:S(2)}, u32[]{:S(2)}) collective-permute-start(f32[1,128]{1,0:T(1,128)S(1)} %add_add_fusion.1), channel_id=1, source_target_pairs={{0,6},{1,7},{2,4},{3,5},{4,2},{5,3},{6,0},{7,1},{8,14},{9,15},{10,... | collective-permute-start | bytes 1544 | tf_op jit(solution)/shard_map/ppermute | solution.py:223
  39.4 0.8 %collective-permute-start.9 = (f32[1,128]{1,0:T(1,128)S(1)}, f32[1,128]{1,0:T(1,128)S(1)}, u32[]{:S(2)}, u32[]{:S(2)}) collective-permute-start(f32[1,128]{1,0:T(1,128)S(1)} %add_add_fusion.1), channel_id=1, source_target_pairs={{0,4},{1,5},{2,6},{3,7},{4,0},{5,1},{6,2},{7,3},{8,12},{9,13},{10,... | collective-permute-start | bytes 1544 | tf_op jit(solution)/shard_map/ppermute | solution.py:223
  40.2 0.6 %collective-permute-start.8 = (f32[1,128]{1,0:T(1,128)S(1)}, f32[1,128]{1,0:T(1,128)S(1)}, u32[]{:S(2)}, u32[]{:S(2)}) collective-permute-start(f32[1,128]{1,0:T(1,128)S(1)} %add_add_fusion.1), channel_id=1, source_target_pairs={{0,2},{1,3},{2,0},{3,1},{4,6},{5,7},{6,4},{7,5},{8,10},{9,11},{10,... | collective-permute-start | bytes 1544 | tf_op jit(solution)/shard_map/ppermute | solution.py:223
  40.9 2.0 %collective-permute-done.9 = f32[1,128]{1,0:T(1,128)S(1)} collective-permute-done((f32[1,128]{1,0:T(1,128)S(1)}, f32[1,128]{1,0:T(1,128)S(1)}, u32[]{:S(2)}, u32[]{:S(2)}) %collective-permute-start.9) | collective-permute-done | bytes 544 | tf_op jit(solution)/shard_map/ppermute | solution.py:223
  42.9 0.8 %collective-permute-done.8 = f32[1,128]{1,0:T(1,128)S(1)} collective-permute-done((f32[1,128]{1,0:T(1,128)S(1)}, f32[1,128]{1,0:T(1,128)S(1)}, u32[]{:S(2)}, u32[]{:S(2)}) %collective-permute-start.8) | collective-permute-done | bytes 544 | tf_op jit(solution)/shard_map/ppermute | solution.py:223
  43.7 1.2 %collective-permute-done.11 = f32[1,128]{1,0:T(1,128)S(1)} collective-permute-done((f32[1,128]{1,0:T(1,128)S(1)}, f32[1,128]{1,0:T(1,128)S(1)}, u32[]{:S(2)}, u32[]{:S(2)}) %collective-permute-start.11) | collective-permute-done | bytes 544 | tf_op jit(solution)/shard_map/ppermute | solution.py:223
  45.1 2.4 %divide_subtract_fusion = (f32[4,16,8,256]{3,2,1,0:T(8,128)}, f32[4,16,8,256]{3,2,1,0:T(8,128)}, f32[4,16,8,256]{3,2,1,0:T(8,128)}) fusion(f32[4,16,8,256]{3,2,1,0:T(8,128)S(1)} %copy-done, f32[4,16,8,256]{3,2,1,0:T(8,128)} %get-tuple-element.11, f32[]{:T(128)} %bitcast.5, f32[4,16,8,256]{3,2,1,0:T(8,128)S(1)} %copy-done.1, f32[4,16,8,256]{3,2,1,0:T(8,128)S(1)} %copy-done.2), kind=kLoop, calls=%fused_computation.2 | loop fusion | flops 1703936 | bytes 3670020 | tf_op jit(solution)/shard_map/sub | solution.py:300
  (27 shorter events, 0.2 us)
Async XLA Ops:
  5.2 14.7 %collective-permute-start.2 = (f32[8,3072]{1,0:T(8,128)}, f32[8,3072]{1,0:T(8,128)S(1)}, u32[]{:S(2)}, u32[]{:S(2)}) collective-permute-start(f32[8,3072]{1,0:T(8,128)} %get-tuple-element.9), channel_id=1, source_target_pairs={{0,8},{8,16},{16,24},{24,0},{1,9},{9,17},{17,25},{25,1},{2,10},{10... | collective-permute-start | bytes 294920 | tf_op jit(solution)/shard_map/ppermute | solution.py:276
  8.3 11.7 %collective-permute-start.4 = (f32[8,3072]{1,0:T(8,128)}, f32[8,3072]{1,0:T(8,128)S(1)}, u32[]{:S(2)}, u32[]{:S(2)}) collective-permute-start(f32[8,3072]{1,0:T(8,128)} %get-tuple-element.10), channel_id=1, source_target_pairs={{0,24},{8,0},{16,8},{24,16},{1,25},{9,1},{17,9},{25,17},{2,26},{10... | collective-permute-start | bytes 294920 | tf_op jit(solution)/shard_map/ppermute | solution.py:276
  10.3 34.7 %copy-start.2 = (f32[4,16,8,256]{3,2,1,0:T(8,128)S(1)}, f32[4,16,8,256]{3,2,1,0:T(8,128)}, u32[]{:S(2)}) copy-start(f32[4,16,8,256]{3,2,1,0:T(8,128)} %param.9) | copy-start | bytes 1572868
  11.7 3.7 %collective-permute-start = (f32[64,256]{1,0:T(8,128)S(1)}, f32[64,256]{1,0:T(8,128)S(1)}, u32[]{:S(2)}, u32[]{:S(2)}) collective-permute-start(f32[64,256]{1,0:T(8,128)S(1)} %bitcast.13), channel_id=1, source_target_pairs={{0,1},{1,2},{2,3},{3,4},{4,5},{5,6},{6,7},{8,9},{9,10},{10,11},{11... | collective-permute-start | bytes 196616 | tf_op jit(solution)/shard_map/ppermute | solution.py:263
  13.2 4.9 %collective-permute-start.1 = (f32[64,256]{1,0:T(8,128)S(1)}, f32[64,256]{1,0:T(8,128)S(1)}, u32[]{:S(2)}, u32[]{:S(2)}) collective-permute-start(f32[64,256]{1,0:T(8,128)S(1)} %bitcast.14), channel_id=1, source_target_pairs={{1,0},{2,1},{3,2},{4,3},{5,4},{6,5},{7,6},{9,8},{10,9},{11,10},{12... | collective-permute-start | bytes 196616 | tf_op jit(solution)/shard_map/ppermute | solution.py:264
  14.5 30.6 %copy-start = (f32[4,16,8,256]{3,2,1,0:T(8,128)S(1)}, f32[4,16,8,256]{3,2,1,0:T(8,128)}, u32[]{:S(2)}) copy-start(f32[4,16,8,256]{3,2,1,0:T(8,128)} %refs_0_.3) | copy-start | bytes 1572868
  14.5 30.6 %copy-start.1 = (f32[4,16,8,256]{3,2,1,0:T(8,128)S(1)}, f32[4,16,8,256]{3,2,1,0:T(8,128)}, u32[]{:S(2)}) copy-start(f32[4,16,8,256]{3,2,1,0:T(8,128)} %param.8) | copy-start | bytes 1572868
  14.5 5.4 %collective-permute-start.3 = (f32[8,2048]{1,0:T(8,128)}, f32[8,2048]{1,0:T(8,128)S(1)}, u32[]{:S(2)}, u32[]{:S(2)}) collective-permute-start(f32[8,2048]{1,0:T(8,128)} %get-tuple-element.8.refs_7_), channel_id=1, source_target_pairs={{0,16},{8,24},{16,0},{24,8},{1,17},{9,25},{17,1},{25,9},{2,18},{10... | collective-permute-start | bytes 196616 | tf_op jit(solution)/shard_map/ppermute | solution.py:276
  15.4 4.5 %copy-start.5 = (f32[64,256]{1,0:T(8,128)}, f32[64,256]{1,0:T(8,128)S(1)}, u32[]{:S(2)}) copy-start(f32[64,256]{1,0:T(8,128)S(1)} %collective-permute-done.refs_5_) | copy-start | bytes 196612
  18.1 1.9 %copy-start.6 = (f32[64,256]{1,0:T(8,128)}, f32[64,256]{1,0:T(8,128)S(1)}, u32[]{:S(2)}) copy-start(f32[64,256]{1,0:T(8,128)S(1)} %collective-permute-done.1.refs_6_) | copy-start | bytes 196612
  19.9 0.6 %copy-start.7 = (f32[8,2048]{1,0:T(8,128)}, f32[8,2048]{1,0:T(8,128)S(1)}, u32[]{:S(2)}) copy-start(f32[8,2048]{1,0:T(8,128)S(1)} %collective-permute-done.3.refs_9_) | copy-start | bytes 196612
  19.9 0.7 %copy-start.3 = (f32[8,3072]{1,0:T(8,128)}, f32[8,3072]{1,0:T(8,128)S(1)}, u32[]{:S(2)}) copy-start(f32[8,3072]{1,0:T(8,128)S(1)} %collective-permute-done.2.refs_8_) | copy-start | bytes 294916
  20.6 0.6 %copy-start.4 = (f32[8,3072]{1,0:T(8,128)}, f32[8,3072]{1,0:T(8,128)S(1)}, u32[]{:S(2)}) copy-start(f32[8,3072]{1,0:T(8,128)S(1)} %collective-permute-done.4.refs_10_) | copy-start | bytes 294916
  26.3 0.6 %copy-start.8 = (f32[1,128]{1,0:T(1,128)S(1)}, f32[1,128]{1,0:T(1,128)}, u32[]{:S(2)}) copy-start(f32[1,128]{1,0:T(1,128)} %get-tuple-element.12) | copy-start | bytes 1540
  26.9 5.4 %collective-permute-start.7 = (f32[1,128]{1,0:T(1,128)S(1)}, f32[1,128]{1,0:T(1,128)S(1)}, u32[]{:S(2)}, u32[]{:S(2)}) collective-permute-start(f32[1,128]{1,0:T(1,128)S(1)} %copy-done.8), channel_id=1, source_target_pairs={{0,24},{8,16},{16,8},{24,0},{1,25},{9,17},{17,9},{25,1},{2,26},{10... | collective-permute-start | bytes 1544 | tf_op jit(solution)/shard_map/ppermute | solution.py:223
  29.4 4.5 %collective-permute-start.6 = (f32[1,128]{1,0:T(1,128)S(1)}, f32[1,128]{1,0:T(1,128)S(1)}, u32[]{:S(2)}, u32[]{:S(2)}) collective-permute-start(f32[1,128]{1,0:T(1,128)S(1)} %copy-done.8), channel_id=1, source_target_pairs={{0,16},{8,24},{16,0},{24,8},{1,17},{9,25},{17,1},{25,9},{2,18},{10... | collective-permute-start | bytes 1544 | tf_op jit(solution)/shard_map/ppermute | solution.py:223
  29.4 4.5 %collective-permute-start.5 = (f32[1,128]{1,0:T(1,128)S(1)}, f32[1,128]{1,0:T(1,128)S(1)}, u32[]{:S(2)}, u32[]{:S(2)}) collective-permute-start(f32[1,128]{1,0:T(1,128)S(1)} %copy-done.8), channel_id=1, source_target_pairs={{0,8},{8,0},{16,24},{24,16},{1,9},{9,1},{17,25},{25,17},{2,10},{10... | collective-permute-start | bytes 1544 | tf_op jit(solution)/shard_map/ppermute | solution.py:223
  33.9 7.1 %collective-permute-start.10 = (f32[1,128]{1,0:T(1,128)S(1)}, f32[1,128]{1,0:T(1,128)S(1)}, u32[]{:S(2)}, u32[]{:S(2)}) collective-permute-start(f32[1,128]{1,0:T(1,128)S(1)} %add_add_fusion.1), channel_id=1, source_target_pairs={{0,6},{1,7},{2,4},{3,5},{4,2},{5,3},{6,0},{7,1},{8,14},{9,15},{10,... | collective-permute-start | bytes 1544 | tf_op jit(solution)/shard_map/ppermute | solution.py:223
  39.4 3.6 %collective-permute-start.9 = (f32[1,128]{1,0:T(1,128)S(1)}, f32[1,128]{1,0:T(1,128)S(1)}, u32[]{:S(2)}, u32[]{:S(2)}) collective-permute-start(f32[1,128]{1,0:T(1,128)S(1)} %add_add_fusion.1), channel_id=1, source_target_pairs={{0,4},{1,5},{2,6},{3,7},{4,0},{5,1},{6,2},{7,3},{8,12},{9,13},{10,... | collective-permute-start | bytes 1544 | tf_op jit(solution)/shard_map/ppermute | solution.py:223
  40.2 3.6 %collective-permute-start.8 = (f32[1,128]{1,0:T(1,128)S(1)}, f32[1,128]{1,0:T(1,128)S(1)}, u32[]{:S(2)}, u32[]{:S(2)}) collective-permute-start(f32[1,128]{1,0:T(1,128)S(1)} %add_add_fusion.1), channel_id=1, source_target_pairs={{0,2},{1,3},{2,0},{3,1},{4,6},{5,7},{6,4},{7,5},{8,10},{9,11},{10,... | collective-permute-start | bytes 1544 | tf_op jit(solution)/shard_map/ppermute | solution.py:223
  43.7 1.2 %collective-permute-start.11 = (f32[1,128]{1,0:T(1,128)S(1)}, f32[1,128]{1,0:T(1,128)S(1)}, u32[]{:S(2)}, u32[]{:S(2)}) collective-permute-start(f32[1,128]{1,0:T(1,128)S(1)} %add_add_fusion), channel_id=1, source_target_pairs={{0,1},{1,0},{2,3},{3,2},{4,5},{5,4},{6,7},{7,6},{8,9},{9,8},{10,11... | collective-permute-start | bytes 1544 | tf_op jit(solution)/shard_map/ppermute | solution.py:223
